TPU v7x, 32 devices: a whole 2x2x4 slice. The times are simulated.
32 devices in a mesh: section: 4 (over x, core), tensor: 8 (over z, y).
Axes of the slice: x: 2, y: 2, z: 4, core: 2. Of those that a mesh axis runs over, the one named last changes fastest.
Arguments:
- tokens: bfloat16 [2, 64, 4096], replicated, may hold values from -6 to 6
- norm_gain: bfloat16 [4, 4096], replicated, may hold values from 0.25 to 1.75
- w_in: bfloat16 [4, 2, 14336, 4096], P('section', None, 'tensor'), may hold values from -0.09375 to 0.09375
- w_out: bfloat16 [4, 14336, 4096], P('section', 'tensor'), may hold values from -0.046875 to 0.046875
- backup_in: bfloat16 [4, 2, 14336, 4096], P('section', None, 'tensor'), may hold values from -0.09375 to 0.09375
- backup_out: bfloat16 [4, 14336, 4096], P('section', None, 'tensor'), may hold values from -0.046875 to 0.046875
- layer_group: int32 [4], replicated, may hold values from 0 to 3, as said below
- token_counts: int32 [2], replicated, may hold values from 1 to 64, as said below
Outputs:
- handed: bfloat16 [4, 2, 64, 4096], P('section', None, 'tensor')
Inputs may be any that keep to these rules, and one draw needn't show every extreme that they name: layer_group[l] is l or l + 1. The layers that move up form one run of consecutive layers, at least one, that starts at the layer of the one group left without any layer; that group is never the last one. `token_counts`: rows of a micro-batch from its count on are padding. One micro-batch is full, with 64 real tokens; the other has at most 32.
All inputs are finite; a program needn't handle non-finite values.
Results may differ from a plain program's by a relative error of at most 0.025.
Values may be sent and summed in bfloat16 or wider, within the bound.
A program may use at most 192 MiB of HBM per device.

v0:
```python
import jax
import jax.numpy as jnp
from jax import lax
from jax.sharding import PartitionSpec as P

NORM_EPS = 0.25


def passed_along(block, axis, distance):
    devices = range(lax.axis_size(axis))
    route = [(i - distance, i) for i in devices if i - distance in devices]
    return lax.ppermute(block, axis, route)


def finish_sum(hidden, w_down):
    partial_value = jnp.dot(hidden, w_down, preferred_element_type=jnp.float32)
    return lax.psum(partial_value.astype(jnp.bfloat16), "tensor").astype(jnp.float32)


def finish_columns(hidden, w_down):
    full_hidden = lax.all_gather(hidden, "tensor", axis=1, tiled=True)
    row_count = full_hidden.shape[0]
    blocks = lax.axis_size("tensor")
    block_width = full_hidden.shape[1] // blocks
    pieces = jnp.einsum(
        "rbf,bfd->brd",
        full_hidden.reshape(row_count, blocks, block_width),
        w_down.reshape(blocks, block_width, w_down.shape[1]),
        preferred_element_type=jnp.float32,
    )
    rounded = lax.optimization_barrier(pieces.astype(jnp.bfloat16))
    column_sum = jnp.sum(rounded.astype(jnp.float32), axis=0)
    return lax.all_gather(column_sum.astype(jnp.bfloat16), "tensor", axis=1, tiled=True).astype(
        column_sum.dtype
    )


def apply_layer(current, gain_row, w_pair, finish, w_down, factor):
    wide_x = current.astype(jnp.float32)
    mean_square = jnp.mean(wide_x * wide_x, axis=1, keepdims=True)
    normed = (wide_x * lax.rsqrt(mean_square + NORM_EPS) * gain_row.astype(jnp.float32)).astype(
        jnp.bfloat16
    )
    gate_part = lax.dot_general(
        normed, w_pair[0], (((1,), (1,)), ((), ())), preferred_element_type=jnp.float32
    )
    up_part = lax.dot_general(
        normed, w_pair[1], (((1,), (1,)), ((), ())), preferred_element_type=jnp.float32
    )
    hidden = (jax.nn.silu(gate_part) * up_part).astype(jnp.bfloat16)
    summed = finish(hidden, w_down)
    return (wide_x + factor * summed).astype(jnp.bfloat16)


def select_entry(values, position):
    places = jnp.arange(values.shape[0], dtype=jnp.int32)
    return jnp.sum(jnp.where(places == position, values, 0))


def shards(tokens, norm_gain, w_in, w_out, backup_in, backup_out, layer_group, token_counts):
    section_id = lax.axis_index("section")
    sections = lax.axis_size("section")
    tensor_id = lax.axis_index("tensor")
    tensors = lax.axis_size("tensor")
    batches = tokens.shape[0]
    tok_rows = tokens.shape[1]
    row_share = tok_rows // tensors
    levels = jnp.arange(layer_group.shape[0], dtype=jnp.int32)
    own_keep = select_entry(layer_group, section_id) == section_id
    moved_in = (
        jnp.sum(
            jnp.where(levels == section_id - 1, (layer_group == section_id).astype(jnp.int32), 0)
        )
        > 0
    )
    prior = jnp.maximum(section_id - 1, 0)
    own_gain = lax.dynamic_index_in_dim(norm_gain, section_id, 0, keepdims=True)
    moved_gain = lax.dynamic_index_in_dim(norm_gain, prior, 0, keepdims=True)
    own_slot = (own_gain, w_in[0], finish_sum, w_out[0], own_keep)
    moved_slot = (moved_gain, backup_in[0], finish_columns, backup_out[0], moved_in)
    layer_slots = [moved_slot, own_slot]
    positions = jnp.arange(tok_rows, dtype=jnp.int32)
    batch_ids = jnp.arange(batches, dtype=jnp.int32)
    handed = jnp.zeros((batches, row_share, tokens.shape[2]), jnp.bfloat16)
    arrived = jnp.zeros(tokens.shape[1:], jnp.bfloat16)
    steps_total = sections + batches - 1
    for step_index in range(steps_total):
        step_mb = step_index - section_id
        clipped = jnp.clip(step_mb, 0, batches - 1)
        fresh_input = lax.dynamic_index_in_dim(tokens, clipped, 0, keepdims=False)
        current = jnp.where(section_id == 0, fresh_input, arrived)
        row_count = select_entry(token_counts, clipped)
        row_keep = (positions < row_count).astype(jnp.float32)[:, None]
        for gain_row, w_pair, finish, w_down, active in layer_slots:
            factor = row_keep * active.astype(jnp.float32)
            current = apply_layer(current, gain_row, w_pair, finish, w_down, factor)
        row_block = lax.dynamic_slice_in_dim(current, tensor_id * row_share, row_share, 0)
        in_range = (step_mb >= 0) & (step_mb < batches)
        slot_mask = (batch_ids == step_mb) & in_range
        handed = jnp.where(slot_mask[:, None, None], row_block[None], handed)
        if step_index + 1 < steps_total:
            arrived = passed_along(current, "section", 1)
    return handed[None]


def solution(mesh):
    return jax.shard_map(
        shards,
        mesh=mesh,
        in_specs=(
            P(),
            P(),
            P("section", None, "tensor", None),
            P("section", "tensor", None),
            P("section", None, "tensor", None),
            P("section", None, "tensor"),
            P(),
            P(),
        ),
        out_specs=P("section", None, "tensor", None),
        check_vma=False,
    )
```

profile of v0, /device:TPU:0, one launch (start us, length us, event | category | flops | bytes accessed | tf_op | source)
XLA Modules:
  0.0 1051.5 jit_solution(10932967524345073013)
XLA Ops:
  16.8 8.7 fusion.142
  28.4 46.9 %all-gather.6.cloned.1.call-done = bf16[64,14336]{1,0:T(8,128)(2,1)} async-done(((bf16[64,1792]{1,0:T(8,128)(2,1)}), bf16[64,14336]{1,0:T(8,128)(2,1)}) %all-gather.6.cloned.1.call-update) | async-done | bytes 1835024 | tf_op jit(solution)/shard_map/all_gather | solution.py:21
  83.6 31.4 %all_gather.31 = bf16[64,4096]{1,0:T(8,128)(2,1)S(1)} all-gather(bf16[64,512]{1,0:T(8,128)(2,1)S(1)} %reduce_sum.216), channel_id=1, replica_groups=mesh['section'=4,'tensor'=8] {'tensor'}, dimensions={1}, use_global_device_ids=true | all-gather | bytes 589824 | tf_op jit(solution)/shard_map/all_gather | solution.py:33
  123.2 14.3 %fusion.70 = bf16[64,4096]{1,0:T(8,128)(2,1)} fusion(bf16[1,1792,4096]{2,1,0:T(8,128)(2,1)} %param.11, bf16[1,2,1792,4096]{3,2,1,0:T(8,128)(2,1)} %param.10, f32[64,1792]{1,0:T(8,128)S(1)} %fusion.28, bf16[64,4096]{1,0:T(8,128)(2,1)S(1)} %get-tuple-element.29, f32[4096]{0:T(1024)S(1)} %bitcast.191, f32[64]{0:T(128)S(1)} %add_rsqrt_fusion.8), kind=kOutput, calls=%fused_computation.70 | convolution fusion | flops 1881047040 | bytes 30884096 | tf_op jit(solution)/shard_map/dot_general | solution.py:16
  139.0 70.0 %all-reduce.6.cloned.1.call-done = bf16[64,4096]{1,0:T(8,128)(2,1)} async-done(((bf16[64,4096]{1,0:T(8,128)(2,1)}), bf16[64,4096]{1,0:T(8,128)(2,1)}) %all-reduce.6.cloned.1.call-update) | async-done | bytes 524304 | tf_op jit(solution)/shard_map/psum | solution.py:17
  221.2 8.6 fusion.139
  230.5 53.2 %all-gather.8.cloned.1.call-done = bf16[64,14336]{1,0:T(8,128)(2,1)} async-done(((bf16[64,1792]{1,0:T(8,128)(2,1)}), bf16[64,14336]{1,0:T(8,128)(2,1)}) %all-gather.8.cloned.1.call-update) | async-done | bytes 1835024 | tf_op jit(solution)/shard_map/all_gather | solution.py:21
  292.1 31.4 %all_gather.33 = bf16[64,4096]{1,0:T(8,128)(2,1)S(1)} all-gather(bf16[64,512]{1,0:T(8,128)(2,1)S(1)} %reduce_sum.221), channel_id=1, replica_groups=mesh['section'=4,'tensor'=8] {'tensor'}, dimensions={1}, use_global_device_ids=true | all-gather | bytes 589824 | tf_op jit(solution)/shard_map/all_gather | solution.py:33
  331.7 14.3 %fusion.73 = bf16[64,4096]{1,0:T(8,128)(2,1)} fusion(bf16[1,1792,4096]{2,1,0:T(8,128)(2,1)} %param.11, bf16[1,2,1792,4096]{3,2,1,0:T(8,128)(2,1)} %param.10, f32[64,1792]{1,0:T(8,128)S(1)} %fusion.26, bf16[64,4096]{1,0:T(8,128)(2,1)S(1)} %get-tuple-element.25, f32[64]{0:T(128)S(1)} %add_rsqrt_fusion.6, f32[4096]{0:T(1024)S(1)} %bitcast.193), kind=kOutput, calls=%fused_computation.71 | convolution fusion | flops 1881047040 | bytes 30884096 | tf_op jit(solution)/shard_map/dot_general | solution.py:16
  346.8 70.6 %all-reduce.8.cloned.1.call-done = bf16[64,4096]{1,0:T(8,128)(2,1)} async-done(((bf16[64,4096]{1,0:T(8,128)(2,1)}), bf16[64,4096]{1,0:T(8,128)(2,1)}) %all-reduce.8.cloned.1.call-update) | async-done | bytes 524304 | tf_op jit(solution)/shard_map/psum | solution.py:17
  429.6 8.6 fusion.136
  439.0 53.1 %all-gather.10.cloned.1.call-done = bf16[64,14336]{1,0:T(8,128)(2,1)} async-done(((bf16[64,1792]{1,0:T(8,128)(2,1)}), bf16[64,14336]{1,0:T(8,128)(2,1)}) %all-gather.10.cloned.1.call-update) | async-done | bytes 1835024 | tf_op jit(solution)/shard_map/all_gather | solution.py:21
  500.5 31.4 %all_gather.35 = bf16[64,4096]{1,0:T(8,128)(2,1)S(1)} all-gather(bf16[64,512]{1,0:T(8,128)(2,1)S(1)} %reduce_sum.225), channel_id=1, replica_groups=mesh['section'=4,'tensor'=8] {'tensor'}, dimensions={1}, use_global_device_ids=true | all-gather | bytes 589824 | tf_op jit(solution)/shard_map/all_gather | solution.py:33
  540.2 14.3 %fusion.76 = bf16[64,4096]{1,0:T(8,128)(2,1)} fusion(bf16[1,1792,4096]{2,1,0:T(8,128)(2,1)} %param.11, bf16[1,2,1792,4096]{3,2,1,0:T(8,128)(2,1)} %param.10, f32[64,1792]{1,0:T(8,128)S(1)} %fusion.24, bf16[64,4096]{1,0:T(8,128)(2,1)S(1)} %get-tuple-element.21, f32[64]{0:T(128)S(1)} %add_rsqrt_fusion.4, f32[4096]{0:T(1024)S(1)} %bitcast.195), kind=kOutput, calls=%fused_computation.72 | convolution fusion | flops 1881047040 | bytes 30884096 | tf_op jit(solution)/shard_map/dot_general | solution.py:16
  555.3 70.5 %all-reduce.10.cloned.1.call-done = bf16[64,4096]{1,0:T(8,128)(2,1)} async-done(((bf16[64,4096]{1,0:T(8,128)(2,1)}), bf16[64,4096]{1,0:T(8,128)(2,1)}) %all-reduce.10.cloned.1.call-update) | async-done | bytes 524304 | tf_op jit(solution)/shard_map/psum | solution.py:17
  647.4 53.3 %all-gather.12.cloned.1.call-done = bf16[64,14336]{1,0:T(8,128)(2,1)} async-done(((bf16[64,1792]{1,0:T(8,128)(2,1)}), bf16[64,14336]{1,0:T(8,128)(2,1)}) %all-gather.12.cloned.1.call-update) | async-done | bytes 1835024 | tf_op jit(solution)/shard_map/all_gather | solution.py:21
  709.0 31.4 %all_gather.37 = bf16[64,4096]{1,0:T(8,128)(2,1)S(1)} all-gather(bf16[64,512]{1,0:T(8,128)(2,1)S(1)} %reduce_sum.229), channel_id=1, replica_groups=mesh['section'=4,'tensor'=8] {'tensor'}, dimensions={1}, use_global_device_ids=true | all-gather | bytes 589824 | tf_op jit(solution)/shard_map/all_gather | solution.py:33
  748.7 14.3 %fusion.79 = bf16[64,4096]{1,0:T(8,128)(2,1)} fusion(bf16[1,1792,4096]{2,1,0:T(8,128)(2,1)} %param.11, bf16[1,2,1792,4096]{3,2,1,0:T(8,128)(2,1)} %param.10, f32[64,1792]{1,0:T(8,128)S(1)} %fusion.22, bf16[64,4096]{1,0:T(8,128)(2,1)S(1)} %get-tuple-element.17, f32[64]{0:T(128)S(1)} %add_rsqrt_fusion.2, f32[4096]{0:T(1024)S(1)} %bitcast.197), kind=kOutput, calls=%fused_computation.73 | convolution fusion | flops 1881047040 | bytes 30884096 | tf_op jit(solution)/shard_map/dot_general | solution.py:16
  763.7 70.7 %all-reduce.12.cloned.1.call-done = bf16[64,4096]{1,0:T(8,128)(2,1)} async-done(((bf16[64,4096]{1,0:T(8,128)(2,1)}), bf16[64,4096]{1,0:T(8,128)(2,1)}) %all-reduce.12.cloned.1.call-update) | async-done | bytes 524304 | tf_op jit(solution)/shard_map/psum | solution.py:17
  846.6 8.6 fusion.130
  856.9 52.2 %all-gather.14.cloned.1.call-done = bf16[64,14336]{1,0:T(8,128)(2,1)} async-done(((bf16[64,1792]{1,0:T(8,128)(2,1)}), bf16[64,14336]{1,0:T(8,128)(2,1)}) %all-gather.14.cloned.1.call-update) | async-done | bytes 1835024 | tf_op jit(solution)/shard_map/all_gather | solution.py:21
  917.5 31.4 %all_gather.39 = bf16[64,4096]{1,0:T(8,128)(2,1)S(1)} all-gather(bf16[64,512]{1,0:T(8,128)(2,1)S(1)} %reduce_sum.233), channel_id=1, replica_groups=mesh['section'=4,'tensor'=8] {'tensor'}, dimensions={1}, use_global_device_ids=true | all-gather | bytes 589824 | tf_op jit(solution)/shard_map/all_gather | solution.py:33
  957.2 14.3 %fusion.82 = bf16[64,4096]{1,0:T(8,128)(2,1)} fusion(bf16[1,1792,4096]{2,1,0:T(8,128)(2,1)} %param.11, bf16[1,2,1792,4096]{3,2,1,0:T(8,128)(2,1)} %param.10, f32[64,1792]{1,0:T(8,128)S(1)} %fusion.20, f32[64,4096]{1,0:T(8,128)S(1)} %get-tuple-element.13, f32[64]{0:T(128)S(1)} %add_rsqrt_fusion, f32[4096]{0:T(1024)S(1)} %bitcast.199), kind=kOutput, calls=%fused_computation.74 | convolution fusion | flops 1880784896 | bytes 31408384 | tf_op jit(solution)/shard_map/dot_general | solution.py:16
  973.2 69.6 %all-reduce.14.cloned.1.call-done = bf16[64,4096]{1,0:T(8,128)(2,1)} async-done(((bf16[64,4096]{1,0:T(8,128)(2,1)}), bf16[64,4096]{1,0:T(8,128)(2,1)}) %all-reduce.14.cloned.1.call-update) | async-done | bytes 524304 | tf_op jit(solution)/shard_map/psum | solution.py:17
  (106 shorter events, 162.6 us)
Async XLA Ops:
  6.5 10.2 copy-start
  6.5 68.7 %all-gather.6.cloned.1.call-start = ((), (), s32[]{:S(2)}) async-start(), calls=%async_computation | async-start | bytes 2064384 | tf_op jit(solution)/shard_map/all_gather | solution.py:21
  16.8 8.8 copy-start.3
  16.8 10.2 copy-start.4
  25.5 183.5 %all-reduce.6.cloned.1.call-start = ((), (), s32[]{:S(2)}) async-start(), calls=%async_computation.1 | async-start | bytes 1048576 | tf_op jit(solution)/shard_map/psum | solution.py:17
  137.6 146.1 %all-gather.8.cloned.1.call-start = ((), (), s32[]{:S(2)}) async-start(), calls=%async_computation.2 | async-start | bytes 2064384 | tf_op jit(solution)/shard_map/all_gather | solution.py:21
  210.2 2.8 collective-permute-start
  229.8 187.6 %all-reduce.8.cloned.1.call-start = ((), (), s32[]{:S(2)}) async-start(), calls=%async_computation.3 | async-start | bytes 1048576 | tf_op jit(solution)/shard_map/psum | solution.py:17
  346.1 146.1 %all-gather.10.cloned.1.call-start = ((), (), s32[]{:S(2)}) async-start(), calls=%async_computation.4 | async-start | bytes 2064384 | tf_op jit(solution)/shard_map/all_gather | solution.py:21
  418.7 2.8 collective-permute-start.1
  438.3 187.6 %all-reduce.10.cloned.1.call-start = ((), (), s32[]{:S(2)}) async-start(), calls=%async_computation.5 | async-start | bytes 1048576 | tf_op jit(solution)/shard_map/psum | solution.py:17
  554.6 146.1 %all-gather.12.cloned.1.call-start = ((), (), s32[]{:S(2)}) async-start(), calls=%async_computation.6 | async-start | bytes 2064384 | tf_op jit(solution)/shard_map/all_gather | solution.py:21
  627.1 1.7 copy-start.1
  627.1 2.8 collective-permute-start.2
  646.8 187.6 %all-reduce.12.cloned.1.call-start = ((), (), s32[]{:S(2)}) async-start(), calls=%async_computation.7 | async-start | bytes 1048576 | tf_op jit(solution)/shard_map/psum | solution.py:17
  763.0 146.1 %all-gather.14.cloned.1.call-start = ((), (), s32[]{:S(2)}) async-start(), calls=%async_computation.8 | async-start | bytes 2064384 | tf_op jit(solution)/shard_map/all_gather | solution.py:21
  835.6 3.1 copy-start.2
  835.6 2.8 collective-permute-start.3
  855.3 187.6 %all-reduce.14.cloned.1.call-start = ((), (), s32[]{:S(2)}) async-start(), calls=%async_computation.9 | async-start | bytes 1048576 | tf_op jit(solution)/shard_map/psum | solution.py:17
Sparse Core Ops, SparseCore 0:
  25.6 49.5 all-gather.5
  137.7 71.1 all-reduce.5
  230.0 53.7 all-gather.7
  346.2 71.1 all-reduce.7
  438.4 53.7 all-gather.9
  554.7 71.1 all-reduce.9
  646.9 53.7 all-gather.11
  763.1 71.1 all-reduce.11
  855.4 53.7 all-gather.13
  971.6 71.1 all-reduce.13
where the time goes:
time: 1060 us; the launch traced here: 1050 us
  waiting for transfers between devices  615 us (58%)
  matrix products  235 us (22%)
  blocking collectives  157 us (15%)
  other arithmetic  20.4 us (2%)
  between operations  15.6 us (1%)
    psum x5, waiting for transfers between devices, finish_sum(): lax.psum(partial_value.astype(jnp.bfloat16), 'tensor').astype(jnp.float32)  351 us
    all_gather x5, waiting for transfers between devices, finish_columns(): full_hidden = lax.all_gather(hidden, 'tensor', axis=1, tiled=True)  259 us
    all_gather x5, blocking collectives, finish_columns(): lax.all_gather(column_sum.astype(jnp.bfloat16), 'tensor', axis=1, tiled=T...  157 us
    dot_general x10, matrix products, apply_layer(): lax.dot_general(normed, w_pair[0], (((1,), (1,)), ((), ())), preferred_el...  78.6 us
    dot_general x5, matrix products, finish_sum(): partial_value = jnp.dot(hidden, w_down, preferred_element_type=jnp.float32)  71.7 us
    dot_general x5, matrix products, apply_layer(): lax.dot_general(normed, w_pair[1], (((1,), (1,)), ((), ())), preferred_el...  43.2 us
    dot_general x5, matrix products, finish_columns(): jnp.einsum('rbf,bfd->brd', full_hidden.reshape(row_count, blocks, block_w...  41.4 us
  transfers between devices with their start and end apart: 14, of which 14 were waited for; matrix products, arithmetic and copies ran while one was open for 1% of the time, Pallas kernels for 0%

commit v1 on v0

--- a/solution.py
+++ b/solution.py
@@ -18,7 +18,14 @@
 
 
 def finish_columns(hidden, w_down):
-    full_hidden = lax.all_gather(hidden, "tensor", axis=1, tiled=True)
+    ring = [hidden]
+    for hop in range(7):
+        ring.append(lax.ppermute(ring[-1], "tensor", [(dev, (dev + 1) % 8) for dev in range(8)]))
+    full_hidden = jnp.roll(
+        jnp.concatenate(ring[::-1], axis=1),
+        (lax.axis_index("tensor") + 1) * ring[0].shape[1],
+        axis=1,
+    )
     row_count = full_hidden.shape[0]
     blocks = lax.axis_size("tensor")
     block_width = full_hidden.shape[1] // blocks

time: 1060 us -> 1150 us (1.085)
  waiting for transfers between devices: 615 us -> 699 us
    ppermute x0 -> x35, waiting for transfers between devices: none -> 319 us  [finish_columns(): lax.ppermute(ring[-1], 'tensor', [(dev, (dev + 1) % 8) for dev in range(8)])]
    all_gather x5 -> x0, waiting for transfers between devices: 259 us -> none  [finish_columns(): full_hidden = lax.all_gather(hidden, 'tensor', axis=1, tiled=True)]
    psum x5, waiting for transfers between devices: 351 us -> 374 us  [finish_sum(): lax.psum(partial_value.astype(jnp.bfloat16), 'tensor').astype(jnp.float32)]
  transfers between devices with their start and end apart: 14 -> 44, of which waited for: 14 -> 44; matrix products, arithmetic and copies ran while one was open for 1% -> 1% of each run, Pallas kernels for 0% -> 0%
where the time goes in v1:
time: 1150 us; the launch traced here: 1140 us
  waiting for transfers between devices  699 us (61%)
  matrix products  229 us (20%)
  blocking collectives  157 us (14%)
  other arithmetic  27.1 us (2%)
  between operations  15.8 us (1%)
  starting transfers between devices  12.8 us (1%)
    psum x5, waiting for transfers between devices, finish_sum(): lax.psum(partial_value.astype(jnp.bfloat16), 'tensor').astype(jnp.float32)  374 us
    ppermute x35, waiting for transfers between devices, finish_columns(): lax.ppermute(ring[-1], 'tensor', [(dev, (dev + 1) % 8) for dev in range(8)])  319 us
    all_gather x5, blocking collectives, finish_columns(): lax.all_gather(column_sum.astype(jnp.bfloat16), 'tensor', axis=1, tiled=T...  157 us
    dot_general x10, matrix products, apply_layer(): lax.dot_general(normed, w_pair[0], (((1,), (1,)), ((), ())), preferred_el...  78.6 us
    dot_general x5, matrix products, finish_sum(): partial_value = jnp.dot(hidden, w_down, preferred_element_type=jnp.float32)  71.7 us
    dot_general x5, matrix products, apply_layer(): lax.dot_general(normed, w_pair[1], (((1,), (1,)), ((), ())), preferred_el...  39.8 us
    dot_general x5, matrix products, finish_columns(): jnp.einsum('rbf,bfd->brd', full_hidden.reshape(row_count, blocks, block_w...  38.8 us
  transfers between devices with their start and end apart: 44, of which 44 were waited for; matrix products, arithmetic and copies ran while one was open for 1% of the time, Pallas kernels for 0%

profile of v1, /device:TPU:0, one launch (start us, length us, event | category | flops | bytes accessed | tf_op | source)
XLA Modules:
  0.0 1142.6 jit_solution(9261591487575793518)
XLA Ops:
  99.8 31.5 %all_gather.15 = bf16[64,4096]{1,0:T(8,128)(2,1)S(1)} all-gather(bf16[64,512]{1,0:T(8,128)(2,1)S(1)} %reduce_sum.216), channel_id=1, replica_groups=mesh['section'=4,'tensor'=8] {'tensor'}, dimensions={1}, use_global_device_ids=true | all-gather | bytes 589824 | tf_op jit(solution)/shard_map/all_gather | solution.py:40
  139.6 14.3 %fusion.70 = bf16[64,4096]{1,0:T(8,128)(2,1)} fusion(bf16[1,1792,4096]{2,1,0:T(8,128)(2,1)} %param.13, bf16[1,2,1792,4096]{3,2,1,0:T(8,128)(2,1)} %param.12, f32[64,1792]{1,0:T(8,128)S(1)} %fusion.28, bf16[64,4096]{1,0:T(8,128)(2,1)S(1)} %get-tuple-element.30, f32[4096]{0:T(1024)S(1)} %bitcast.191, f32[64]{0:T(128)S(1)} %add_rsqrt_fusion.8), kind=kOutput, calls=%fused_computation.70 | convolution fusion | flops 1881047040 | bytes 30884096 | tf_op jit(solution)/shard_map/dot_general | solution.py:16
  155.3 68.8 %all-reduce.6.cloned.1.call-done = bf16[64,4096]{1,0:T(8,128)(2,1)} async-done(((bf16[64,4096]{1,0:T(8,128)(2,1)}), bf16[64,4096]{1,0:T(8,128)(2,1)}) %all-reduce.6.cloned.1.call-update) | async-done | bytes 524304 | tf_op jit(solution)/shard_map/psum | solution.py:17
  279.3 9.9 collective-permute-done.12
  289.2 11.1 collective-permute-done.13
  320.3 31.2 %all_gather.16 = bf16[64,4096]{1,0:T(8,128)(2,1)S(1)} all-gather(bf16[64,512]{1,0:T(8,128)(2,1)S(1)} %reduce_sum.221), channel_id=1, replica_groups=mesh['section'=4,'tensor'=8] {'tensor'}, dimensions={1}, use_global_device_ids=true | all-gather | bytes 589824 | tf_op jit(solution)/shard_map/all_gather | solution.py:40
  359.7 14.3 %fusion.73 = bf16[64,4096]{1,0:T(8,128)(2,1)} fusion(bf16[1,1792,4096]{2,1,0:T(8,128)(2,1)} %param.13, bf16[1,2,1792,4096]{3,2,1,0:T(8,128)(2,1)} %param.12, f32[64,1792]{1,0:T(8,128)S(1)} %fusion.26, bf16[64,4096]{1,0:T(8,128)(2,1)S(1)} %get-tuple-element.26, f32[64]{0:T(128)S(1)} %add_rsqrt_fusion.6, f32[4096]{0:T(1024)S(1)} %bitcast.193), kind=kOutput, calls=%fused_computation.71 | convolution fusion | flops 1881047040 | bytes 30884096 | tf_op jit(solution)/shard_map/dot_general | solution.py:16
  374.7 76.5 %all-reduce.8.cloned.1.call-done = bf16[64,4096]{1,0:T(8,128)(2,1)} async-done(((bf16[64,4096]{1,0:T(8,128)(2,1)}), bf16[64,4096]{1,0:T(8,128)(2,1)}) %all-reduce.8.cloned.1.call-update) | async-done | bytes 524304 | tf_op jit(solution)/shard_map/psum | solution.py:17
  506.4 9.9 collective-permute-done.20
  516.4 11.1 collective-permute-done.21
  547.2 31.4 %all_gather.17 = bf16[64,4096]{1,0:T(8,128)(2,1)S(1)} all-gather(bf16[64,512]{1,0:T(8,128)(2,1)S(1)} %reduce_sum.225), channel_id=1, replica_groups=mesh['section'=4,'tensor'=8] {'tensor'}, dimensions={1}, use_global_device_ids=true | all-gather | bytes 589824 | tf_op jit(solution)/shard_map/all_gather | solution.py:40
  586.8 14.3 %fusion.76 = bf16[64,4096]{1,0:T(8,128)(2,1)} fusion(bf16[1,1792,4096]{2,1,0:T(8,128)(2,1)} %param.13, bf16[1,2,1792,4096]{3,2,1,0:T(8,128)(2,1)} %param.12, f32[64,1792]{1,0:T(8,128)S(1)} %fusion.24, bf16[64,4096]{1,0:T(8,128)(2,1)S(1)} %get-tuple-element.22, f32[64]{0:T(128)S(1)} %add_rsqrt_fusion.4, f32[4096]{0:T(1024)S(1)} %bitcast.195), kind=kOutput, calls=%fused_computation.72 | convolution fusion | flops 1881047040 | bytes 30884096 | tf_op jit(solution)/shard_map/dot_general | solution.py:16
  601.9 76.4 %all-reduce.10.cloned.1.call-done = bf16[64,4096]{1,0:T(8,128)(2,1)} async-done(((bf16[64,4096]{1,0:T(8,128)(2,1)}), bf16[64,4096]{1,0:T(8,128)(2,1)}) %all-reduce.10.cloned.1.call-update) | async-done | bytes 524304 | tf_op jit(solution)/shard_map/psum | solution.py:17
  733.5 9.9 collective-permute-done.28
  743.5 11.1 collective-permute-done.29
  774.5 31.2 %all_gather.18 = bf16[64,4096]{1,0:T(8,128)(2,1)S(1)} all-gather(bf16[64,512]{1,0:T(8,128)(2,1)S(1)} %reduce_sum.229), channel_id=1, replica_groups=mesh['section'=4,'tensor'=8] {'tensor'}, dimensions={1}, use_global_device_ids=true | all-gather | bytes 589824 | tf_op jit(solution)/shard_map/all_gather | solution.py:40
  813.9 14.4 %fusion.79 = bf16[64,4096]{1,0:T(8,128)(2,1)} fusion(bf16[1,1792,4096]{2,1,0:T(8,128)(2,1)} %param.13, bf16[1,2,1792,4096]{3,2,1,0:T(8,128)(2,1)} %param.12, f32[64,1792]{1,0:T(8,128)S(1)} %fusion.22, bf16[64,4096]{1,0:T(8,128)(2,1)S(1)} %get-tuple-element.18, f32[64]{0:T(128)S(1)} %add_rsqrt_fusion.2, f32[4096]{0:T(1024)S(1)} %bitcast.197), kind=kOutput, calls=%fused_computation.73 | convolution fusion | flops 1881047040 | bytes 30884096 | tf_op jit(solution)/shard_map/dot_general | solution.py:16
  829.0 76.5 %all-reduce.12.cloned.1.call-done = bf16[64,4096]{1,0:T(8,128)(2,1)} async-done(((bf16[64,4096]{1,0:T(8,128)(2,1)}), bf16[64,4096]{1,0:T(8,128)(2,1)}) %all-reduce.12.cloned.1.call-update) | async-done | bytes 524304 | tf_op jit(solution)/shard_map/psum | solution.py:17
  960.8 9.9 collective-permute-done.36
  970.8 11.3 collective-permute-done.37
  982.1 10.3 collective-permute-done.38
  1002.7 31.5 %all_gather.19 = bf16[64,4096]{1,0:T(8,128)(2,1)S(1)} all-gather(bf16[64,512]{1,0:T(8,128)(2,1)S(1)} %reduce_sum.233), channel_id=1, replica_groups=mesh['section'=4,'tensor'=8] {'tensor'}, dimensions={1}, use_global_device_ids=true | all-gather | bytes 589824 | tf_op jit(solution)/shard_map/all_gather | solution.py:40
  1042.5 14.4 %fusion.82 = bf16[64,4096]{1,0:T(8,128)(2,1)} fusion(bf16[1,1792,4096]{2,1,0:T(8,128)(2,1)} %param.13, bf16[1,2,1792,4096]{3,2,1,0:T(8,128)(2,1)} %param.12, f32[64,1792]{1,0:T(8,128)S(1)} %fusion.20, f32[64,4096]{1,0:T(8,128)S(1)} %get-tuple-element.14, f32[64]{0:T(128)S(1)} %add_rsqrt_fusion, f32[4096]{0:T(1024)S(1)} %bitcast.199), kind=kOutput, calls=%fused_computation.74 | convolution fusion | flops 1880784896 | bytes 31408384 | tf_op jit(solution)/shard_map/dot_general | solution.py:16
  1057.7 76.2 %all-reduce.14.cloned.1.call-done = bf16[64,4096]{1,0:T(8,128)(2,1)} async-done(((bf16[64,4096]{1,0:T(8,128)(2,1)}), bf16[64,4096]{1,0:T(8,128)(2,1)}) %all-reduce.14.cloned.1.call-update) | async-done | bytes 524304 | tf_op jit(solution)/shard_map/psum | solution.py:17
  (204 shorter events, 429.4 us)
Async XLA Ops:
  6.5 217.5 %all-reduce.6.cloned.1.call-start = ((), (), s32[]{:S(2)}) async-start(), calls=%async_computation | async-start | bytes 1048576 | tf_op jit(solution)/shard_map/psum | solution.py:17
  24.7 11.7 %collective-permute-start = (bf16[64,1792]{1,0:T(8,128)(2,1)S(1)}, bf16[64,1792]{1,0:T(8,128)(2,1)S(1)}, u32[]{:S(2)}, u32[]{:S(2)}) collective-permute-start(bf16[64,1792]{1,0:T(8,128)(2,1)S(1)} %fusion.142), channel_id=1, source_target_pairs={{0,1},{1,2},{2,3},{3,4},{4,5},{5,6},{6,7},{7,0},{8,9},{9,10},{10,1... | collective-permute-start | bytes 688136 | tf_op jit(solution)/shard_map/ppermute | solution.py:23
  36.4 9.5 collective-permute-start.1
  72.0 9.6 collective-permute-start.5
  153.9 297.3 %all-reduce.8.cloned.1.call-start = ((), (), s32[]{:S(2)}) async-start(), calls=%async_computation.1 | async-start | bytes 1048576 | tf_op jit(solution)/shard_map/psum | solution.py:17
  270.5 8.8 collective-permute-start.11
  279.3 10.0 collective-permute-start.12
  289.2 11.1 collective-permute-start.13
  300.3 10.6 collective-permute-start.14
  374.1 304.2 %all-reduce.10.cloned.1.call-start = ((), (), s32[]{:S(2)}) async-start(), calls=%async_computation.2 | async-start | bytes 1048576 | tf_op jit(solution)/shard_map/psum | solution.py:17
  497.6 8.8 collective-permute-start.19
  506.4 9.9 collective-permute-start.20
  516.4 11.1 collective-permute-start.21
  527.4 10.3 collective-permute-start.22
  601.2 304.3 %all-reduce.12.cloned.1.call-start = ((), (), s32[]{:S(2)}) async-start(), calls=%async_computation.3 | async-start | bytes 1048576 | tf_op jit(solution)/shard_map/psum | solution.py:17
  724.7 8.8 collective-permute-start.27
  733.5 9.9 collective-permute-start.28
  743.5 11.1 collective-permute-start.29
  754.6 10.5 collective-permute-start.30
  828.3 305.6 %all-reduce.14.cloned.1.call-start = ((), (), s32[]{:S(2)}) async-start(), calls=%async_computation.4 | async-start | bytes 1048576 | tf_op jit(solution)/shard_map/psum | solution.py:17
  951.9 8.8 collective-permute-start.35
  960.7 10.1 collective-permute-start.36
  970.8 11.3 collective-permute-start.37
  982.1 10.3 collective-permute-start.38
  (24 other events, 291.6 us)
Sparse Core Ops, SparseCore 0:
  154.0 69.9 all-reduce.5
  374.2 76.9 all-reduce.7
  601.3 76.9 all-reduce.9
  828.4 77.0 all-reduce.11
  1057.0 76.8 all-reduce.13
